TPU v7x, 256 devices: a whole 4x4x8 slice. The times are simulated.
256 devices in a mesh: dp: 4 (over y), expert: 32 (over x, z), etp: 2 (over core).
Axes of the slice: x: 4, y: 4, z: 8, core: 2. Of those that a mesh axis runs over, the one named last changes fastest.
Arguments:
- tokens: bfloat16 [8192, 4096], P(('dp', 'expert'), 'etp'), may hold values from -6 to 6
- expert_ids: int32 [8192, 8], P(('dp', 'expert')), may hold values from 0 to 63, all different within a row; in each aligned block of 64 rows (0 to 63, 64 to 127, ...) at most 12 rows name the same one
- combine: float32 [8192, 8], P(('dp', 'expert')), may hold values from 0.05 to 1
- gate_weight: bfloat16 [64, 4096, 1536], P('expert', 'dp', 'etp'), may hold values from -0.09375 to 0.09375
- up_weight: bfloat16 [64, 4096, 1536], P('expert', 'dp', 'etp'), may hold values from -0.09375 to 0.09375
- down_weight: bfloat16 [64, 1536, 4096], P('expert', 'etp', 'dp'), may hold values from -0.15625 to 0.15625
Outputs:
- mixed: bfloat16 [8192, 4096], P(('dp', 'expert'), 'etp')
Inputs may be any that keep to these rules, and one draw needn't show every extreme that they name: `expert_ids`: each row names 8 different experts. In the rows of one device (aligned blocks of 64 rows) no expert is named by more than 12 rows, a bound that some block reaches.
All inputs are finite; a program needn't handle non-finite values.
Results may differ from a plain program's by a relative error of at most 0.008.
Values may be sent and summed in bfloat16 or wider, within the bound.
No kernel may reach another device: no remote copies, remote signals or barrier semaphores. Data moves between devices by JAX's collectives and lax.ppermute only.
A program may use at most 192 MiB of HBM per device.

v0:
```python
import jax
import jax.numpy as jnp
from jax import lax
from jax.sharding import PartitionSpec as P


def sent_to_all(shard, axis):
    copies = jnp.broadcast_to(shard, (lax.axis_size(axis), *shard.shape))
    return lax.all_to_all(copies, axis, split_axis=0, concat_axis=0, tiled=True)


def laid_out(pieces, dim):
    pieces = jnp.moveaxis(pieces, 0, dim)
    dims = pieces.shape
    return pieces.reshape(*dims[:dim], dims[dim] * dims[dim + 1], *dims[dim + 2 :])


def gather_directly(shard, axis, dim):
    pieces = sent_to_all(shard, axis)
    return laid_out(pieces, dim)


def in_one_piece(arrays, axis, dim, along):
    widths = [a.shape[along] for a in arrays]
    both = jnp.concatenate(arrays, axis=along)
    filled = lax.all_gather(both, axis, axis=dim, tiled=True)
    return tuple(jnp.split(filled, [sum(widths[:k]) for k in range(1, len(widths))], axis=along))


def cut_along(shard, dim, count):
    before, after = (shard.shape[:dim], shard.shape[dim + 1 :])
    return jnp.moveaxis(shard.reshape(*before, count, -1, *after), dim, 0)


def sum_at_owner(shard, axis, dim):
    count = lax.axis_size(axis)
    pieces = lax.all_to_all(cut_along(shard, dim, count), axis, 0, 0, tiled=True)
    return jnp.sum(pieces.astype(jnp.float32), axis=0)


def shards(tokens, expert_ids, combine, gate_weight, up_weight, down_weight):
    tok_rows, top_count = expert_ids.shape
    held_count = gate_weight.shape[0]
    groups = lax.axis_size("expert")
    experts = held_count * groups
    capacity = min(tok_rows, 3 * tok_rows * top_count // (2 * experts))
    slots_all = experts * capacity
    onehot = (expert_ids[:, :, None] == jnp.arange(experts, dtype=jnp.int32)[None, None, :]).astype(
        jnp.int32
    )
    flattened = onehot.reshape(tok_rows * top_count, experts)
    before = jnp.cumsum(flattened, axis=0) - flattened
    slot_index = jnp.sum(before * flattened, axis=1).reshape(tok_rows, top_count)
    target = expert_ids * capacity + slot_index
    matches = target[:, :, None] == jnp.arange(slots_all, dtype=jnp.int32)[None, None, :]
    picker = jnp.any(matches, axis=1).astype(jnp.bfloat16)
    weights_map = jnp.sum(jnp.where(matches, combine[:, :, None], 0.0), axis=1)
    gathered = gather_directly(tokens, "etp", 1)
    packed = jnp.einsum("ts,td->sd", picker, gathered, preferred_element_type=jnp.float32).astype(
        jnp.bfloat16
    )
    arrived = lax.all_to_all(
        packed.reshape(groups, held_count, capacity, gathered.shape[1]),
        "expert",
        split_axis=0,
        concat_axis=2,
        tiled=True,
    )
    inputs = arrived[0]
    pieces = in_one_piece((gate_weight, up_weight), "dp", 1, 0)
    gate_part = jnp.einsum("erd,edf->erf", inputs, pieces[0], preferred_element_type=jnp.float32)
    up_part = jnp.einsum("erd,edf->erf", inputs, pieces[1], preferred_element_type=jnp.float32)
    hidden = (jax.nn.silu(gate_part) * up_part).astype(jnp.bfloat16)
    partial_value = jnp.einsum(
        "erf,efd->erd",
        hidden,
        lax.all_gather(down_weight, "dp", axis=2, tiled=True),
        preferred_element_type=jnp.float32,
    ).astype(jnp.bfloat16)
    partial_value = lax.optimization_barrier(partial_value)
    summed = sum_at_owner(partial_value.astype(jnp.float32).astype(jnp.bfloat16), "etp", 2)
    expert_out = summed.astype(jnp.bfloat16)
    returned_rows = lax.all_to_all(
        expert_out[None], "expert", split_axis=2, concat_axis=0, tiled=True
    )
    returned_rows = returned_rows.reshape(slots_all, returned_rows.shape[3])
    weight_high = weights_map.astype(jnp.bfloat16)
    weight_low = (weights_map - weight_high.astype(jnp.float32)).astype(jnp.bfloat16)
    result = jnp.dot(weight_high, returned_rows, preferred_element_type=jnp.float32)
    result = result + jnp.dot(weight_low, returned_rows, preferred_element_type=jnp.float32)
    return result.astype(jnp.bfloat16)


def solution(mesh):
    placed = (
        P(("dp", "expert"), "etp"),
        P(("dp", "expert"), None),
        P(("dp", "expert"), None),
        P("expert", "dp", "etp"),
        P("expert", "dp", "etp"),
        P("expert", "etp", "dp"),
    )
    return jax.shard_map(
        shards, mesh=mesh, in_specs=placed, out_specs=P(("dp", "expert"), "etp"), check_vma=False
    )
```

profile of v0, /device:TPU:8, one launch (start us, length us, event | category | flops | bytes accessed | tf_op | source)
XLA Modules:
  0.0 497.5 jit_solution(5117173287641867535)
XLA Ops:
  6.5 6.0 %pad_maximum_fusion = bf16[4,1024,768]{2,1,0:T(8,128)(2,1)} fusion(bf16[2,1024,768]{2,1,0:T(8,128)(2,1)} %param.10, bf16[2,1024,768]{2,1,0:T(8,128)(2,1)} %param.9), kind=kLoop, calls=%fused_computation.7 | loop fusion | flops 3145728 | bytes 12582912 | tf_op jit(solution)/shard_map/concatenate | solution.py:25
  12.6 0.7 all-gather.5.cloned.1.call-update
  13.3 0.2 copy-done.1
  13.5 0.9 broadcast_in_dim.25
  14.4 3.5 all-to-all-start
  18.0 0.1 eq.43
  18.1 0.1 eq.39
  18.2 1.2 reduce-window.6
  19.4 0.2 slice_reduce_fusion
  19.7 0.1 fusion.14
  19.8 0.1 reshape.38
  20.1 0.5 fusion.11
  20.6 4.4 convolution_convert_fusion.1
  25.1 10.3 %reshape.40 = bf16[32,2,12,4096]{3,2,1,0:T(8,128)(2,1)} reshape(bf16[768,4096]{1,0:T(8,128)(2,1)} %convolution_convert_fusion.1) | data formatting | bytes 12582912 | tf_op jit(solution)/shard_map/reshape | solution.py:63
  35.3 9.9 %copy.54 = bf16[32,2,12,4096]{3,1,2,0:T(2,128)(2,1)S(1)} copy(bf16[32,2,12,4096]{3,2,1,0:T(8,128)(2,1)} %reshape.40) | data formatting | bytes 12582912 | tf_op jit(solution)/shard_map/reshape | solution.py:63
  45.2 153.1 %all_to_all.40 = bf16[32,2,12,4096]{3,1,2,0:T(2,128)(2,1)} all-to-all(bf16[32,2,12,4096]{3,1,2,0:T(2,128)(2,1)S(1)} %copy.54), channel_id=1, replica_groups=mesh['dp'=4,'expert'=32,'etp'=2] {'expert'}, dimensions={0} | all-to-all | bytes 12582912 | tf_op jit(solution)/shard_map/all_to_all | solution.py:62
  198.3 43.2 %all-gather.3.cloned.1.call-done = bf16[4,4096,768]{2,1,0:T(8,128)(2,1)} async-done(((bf16[4,1024,768]{2,1,0:T(8,128)(2,1)}), bf16[4,4096,768]{2,1,0:T(8,128)(2,1)}) %all-gather.3.cloned.1.call-update) | async-done | bytes 25165840 | tf_op jit(solution)/shard_map/all_gather | solution.py:26
  241.6 17.3 %fusion.2 = f32[2,384,768]{2,1,0:T(8,128)} fusion(bf16[4,4096,768]{2,1,0:T(8,128)(2,1)} %all-gather.3.cloned.1.call-done, bf16[2,384,4096]{2,0,1:T(2,128)(2,1)} %bitcast.50), kind=kOutput, calls=%fused_computation.2 | convolution fusion | flops 4831838208 | bytes 21233664 | tf_op jit(solution)/shard_map/erd,edf->erf/dot_general | solution.py:71
  258.9 16.0 %multiply_convert_fusion = bf16[2,384,768]{2,1,0:T(8,128)(2,1)} fusion(f32[2,384,768]{2,1,0:T(8,128)} %fusion.2, bf16[4,4096,768]{2,1,0:T(8,128)(2,1)} %all-gather.3.cloned.1.call-done, bf16[2,384,4096]{2,0,1:T(2,128)(2,1)S(1)} %bitcast.51), kind=kOutput, calls=%fused_computation.10 | convolution fusion | flops 4835377152 | bytes 22413312 | tf_op jit(solution)/shard_map/erd,edf->erf/dot_general | solution.py:72
  274.9 90.6 %all-gather.5.cloned.1.call-done = bf16[2,768,4096]{2,1,0:T(8,128)(2,1)} async-done(((bf16[2,768,1024]{2,1,0:T(8,128)(2,1)}), bf16[2,768,4096]{2,1,0:T(8,128)(2,1)}) %all-gather.5.cloned.1.call-update) | async-done | bytes 12582928 | tf_op jit(solution)/shard_map/all_gather | solution.py:77
  365.5 8.4 %convolution_convert_fusion = bf16[2,384,4096]{2,1,0:T(8,128)(2,1)S(1)} fusion(bf16[2,384,768]{2,1,0:T(8,128)(2,1)} %multiply_convert_fusion, bf16[2,768,4096]{2,1,0:T(8,128)(2,1)} %all-gather.5.cloned.1.call-done), kind=kOutput, calls=%fused_computation.4 | convolution fusion | flops 4834983936 | bytes 20054016 | tf_op jit(solution)/shard_map/erf,efd->erd/dot_general | solution.py:74
  373.9 1.1 copy.73
  375.0 10.0 %all_to_all.41 = bf16[2,2,384,2048]{3,2,1,0:T(8,128)(2,1)} all-to-all(bf16[2,2,384,2048]{3,2,1,0:T(8,128)(2,1)S(1)} %bitcast.47), channel_id=1, replica_groups=mesh['dp'=4,'expert'=32,'etp'=2] {'etp'}, dimensions={0} | all-to-all | bytes 12582912 | tf_op jit(solution)/shard_map/all_to_all | solution.py:37
  385.0 5.4 %reduce_sum.32 = bf16[2,384,2048]{2,1,0:T(8,128)(2,1)S(1)} reduce(bf16[2,2,384,2048]{3,2,1,0:T(8,128)(2,1)} %all_to_all.41, bf16[]{:T(256)} %constant.16.clone.1), dimensions={0}, to_apply=%region_5.6 | reduce | flops 1572864 | bytes 9437186 | tf_op jit(solution)/shard_map/reduce_sum | solution.py:38
  390.4 4.9 copy.59
  395.3 9.9 %all-to-all-start.3 = ((bf16[1,2,384,2048]{3,1,0,2:T(2,128)(2,1)}), bf16[1,2,384,2048]{3,1,0,2:T(2,128)(2,1)S(1)}, u32[]{:S(2)}, u32[]{:S(2)}) async-start(bf16[1,2,384,2048]{3,1,0,2:T(2,128)(2,1)} %copy.59), calls=%async_computation.3 | async-start | bytes 6291456 | tf_op jit(solution)/shard_map/all_to_all | solution.py:83
  405.4 0.5 select_reduce_fusion
  406.0 74.4 %all-to-all-done.3 = bf16[1,2,384,2048]{3,1,0,2:T(2,128)(2,1)S(1)} async-done(((bf16[1,2,384,2048]{3,1,0,2:T(2,128)(2,1)}), bf16[1,2,384,2048]{3,1,0,2:T(2,128)(2,1)S(1)}, u32[]{:S(2)}, u32[]{:S(2)}) %all-to-all-start.3) | async-done | bytes 3145760 | tf_op jit(solution)/shard_map/all_to_all | solution.py:83
  480.3 3.5 copy.60
  483.9 4.7 reshape.42
  488.6 0.7 fusion.17
  489.2 1.4 fusion.6
  (20 shorter events, 0.5 us)
Async XLA Ops:
  6.5 235.0 %all-gather.3.cloned.1.call-start = ((), (), s32[]{:S(2)}) async-start(), calls=%async_computation.4 | async-start | bytes 31457280 | tf_op jit(solution)/shard_map/all_gather | solution.py:26
  12.6 1.0 copy-start.1
  12.6 5.3 %copy-start.2 = (s32[64,8]{0,1:T(8,128)S(1)}, s32[64,8]{0,1:T(8,128)}, u32[]{:S(2)}) copy-start(s32[64,8]{0,1:T(8,128)} %param.7) | copy-start | bytes 6148
  12.6 352.9 %all-gather.5.cloned.1.call-start = ((), (), s32[]{:S(2)}) async-start(), calls=%async_computation.5 | async-start | bytes 15728640 | tf_op jit(solution)/shard_map/all_gather | solution.py:77
  14.4 5.7 %all-to-all-start = ((bf16[2,64,2048]{2,1,0:T(8,128)(2,1)}), bf16[2,64,2048]{2,1,0:T(8,128)(2,1)S(1)}, u32[]{:S(2)}, u32[]{:S(2)}) async-start(bf16[2,64,2048]{2,1,0:T(8,128)(2,1)} %broadcast_in_dim.25), calls=%async_computation | async-start | bytes 1048576 | tf_op jit(solution)/shard_map/all_to_all | solution.py:9
  241.5 17.3 %copy-start = (bf16[32,2,12,4096]{3,1,2,0:T(2,128)(2,1)S(1)}, bf16[32,2,12,4096]{3,1,2,0:T(2,128)(2,1)}, u32[]{:S(2)}) copy-start(bf16[32,2,12,4096]{3,1,2,0:T(2,128)(2,1)} %all_to_all.40) | copy-start | bytes 18874372
  395.3 10.0 %copy-start.3 = (f32[64,8]{0,1:T(8,128)S(1)}, f32[64,8]{0,1:T(8,128)}, u32[]{:S(2)}) copy-start(f32[64,8]{0,1:T(8,128)} %param.8) | copy-start | bytes 6148
  395.3 85.0 %all-to-all-start.3 = ((bf16[1,2,384,2048]{3,1,0,2:T(2,128)(2,1)}), bf16[1,2,384,2048]{3,1,0,2:T(2,128)(2,1)S(1)}, u32[]{:S(2)}, u32[]{:S(2)}) async-start(bf16[1,2,384,2048]{3,1,0,2:T(2,128)(2,1)} %copy.59), calls=%async_computation.3 | async-start | bytes 6291456 | tf_op jit(solution)/shard_map/all_to_all | solution.py:83
Sparse Core Ops, SparseCore 0:
  12.7 228.8 all-gather.2
  243.4 122.0 all-gather.4
where the time goes:
time: 498 us; the launch traced here: 497 us
  waiting for transfers between devices  209 us (42%)
  blocking collectives  163 us (33%)
  matrix products  48.2 us (10%)
  local copies, waits for them, and re-layouts  36.3 us (7%)
  other arithmetic  13.9 us (3%)
  between operations  13.6 us (3%)
  starting transfers between devices  13.5 us (3%)
    all_to_all x1, blocking collectives, shards(): lax.all_to_all(packed.reshape(groups, held_count, capacity, gathered.shap...  153 us
    all_gather x1, waiting for transfers between devices, shards(): lax.all_gather(down_weight, 'dp', axis=2, tiled=True)  90.6 us
    all_to_all x1, waiting for transfers between devices, shards(): lax.all_to_all(expert_out[None], 'expert', split_axis=2, concat_axis=0, t...  74.4 us
    all_gather x1, waiting for transfers between devices, in_one_piece(): filled = lax.all_gather(both, axis, axis=dim, tiled=True)  43.2 us
    reshape x2, local copies, waits for them, and re-layouts, shards(): packed.reshape(groups, held_count, capacity, gathered.shape[1])  20.2 us
    dot_general x1, matrix products, shards(): jnp.einsum('erd,edf->erf', inputs, pieces[0], preferred_element_type=jnp....  17.3 us
    dot_general x1, matrix products, shards(): jnp.einsum('erd,edf->erf', inputs, pieces[1], preferred_element_type=jnp....  16 us
    all_to_all x1, blocking collectives, sum_at_owner(): lax.all_to_all(cut_along(shard, dim, count), axis, 0, 0, tiled=True)  9.99 us
  transfers between devices with their start and end apart: 4, of which 3 were waited for; matrix products, arithmetic and copies ran while one was open for 12% of the time, Pallas kernels for 0%

commit v1 on v0

--- a/solution.py
+++ b/solution.py
@@ -1,7 +1,20 @@
+import functools
 import jax
 import jax.numpy as jnp
 from jax import lax
 from jax.sharding import PartitionSpec as P
+
+
+def convert_sums_all_in(my_tile, array_dim):
+    return jnp.concatenate(
+        lax.all_to_all(
+            jnp.stack([my_tile for _ in range(lax.axis_size("dp"))], axis=0), "dp", 0, 0
+        ),
+        axis=array_dim,
+    )
+
+
+_compute_bands = functools.partial(convert_sums_all_in, array_dim=2)
 
 
 def sent_to_all(shard, axis):
@@ -72,10 +85,7 @@
     up_part = jnp.einsum("erd,edf->erf", inputs, pieces[1], preferred_element_type=jnp.float32)
     hidden = (jax.nn.silu(gate_part) * up_part).astype(jnp.bfloat16)
     partial_value = jnp.einsum(
-        "erf,efd->erd",
-        hidden,
-        lax.all_gather(down_weight, "dp", axis=2, tiled=True),
-        preferred_element_type=jnp.float32,
+        "erf,efd->erd", hidden, _compute_bands(down_weight), preferred_element_type=jnp.float32
     ).astype(jnp.bfloat16)
     partial_value = lax.optimization_barrier(partial_value)
     summed = sum_at_owner(partial_value.astype(jnp.float32).astype(jnp.bfloat16), "etp", 2)

time: 498 us -> 625 us (1.26)
  waiting for transfers between devices: 209 us -> 446 us
  blocking collectives: 163 us -> 15 us
  local copies, waits for them, and re-layouts: 36.3 us -> 53.6 us
  starting transfers between devices: 13.5 us -> 27.9 us
    all_to_all x1 -> x2, waiting for transfers between devices: 0.01 us -> 371 us  [the longest x1 244 us: convert_sums_all_in(): lax.all_to_all(jnp.stack([my_tile for _ in range(lax.axis_size('dp'))], a...]
    all_to_all x1, blocking collectives: 153 us -> 5.03 us  [sent_to_all(): return lax.all_to_all(copies, axis, split_axis=0, concat_axis=0, tiled=True)]
    all_gather x1 -> x0, waiting for transfers between devices: 90.6 us -> none  [shards(): lax.all_gather(down_weight, 'dp', axis=2, tiled=True)]
    all_gather x1, waiting for transfers between devices: 43.2 us -> 0.01 us  [in_one_piece(): filled = lax.all_gather(both, axis, axis=dim, tiled=True)]
    all_to_all x1 -> x2, starting transfers between devices: 3.49 us -> 19.6 us  [the longest x1 9.84 us: shards(): lax.all_to_all(packed.reshape(groups, held_count, capacity, gathered.shap...]
    reshape x0 -> x1, local copies, waits for them, and re-layouts: none -> 10.7 us  [convert_sums_all_in(): jnp.concatenate(lax.all_to_all(jnp.stack([my_tile for _ in range(lax.axis...]
    another operation x1 -> x2, local copies, waits for them, and re-layouts: 0.01 us -> 6.32 us  [the longest x1 6.32 us: convert_sums_all_in(): jnp.stack([my_tile for _ in range(lax.axis_size('dp'))], axis=0)]
  transfers between devices with their start and end apart: 4 -> 4, of which waited for: 3 -> 3; matrix products, arithmetic and copies ran while one was open for 12% -> 7% of each run, Pallas kernels for 0% -> 0%
where the time goes in v1:
time: 625 us; the launch traced here: 622 us
  waiting for transfers between devices  446 us (71%)
  local copies, waits for them, and re-layouts  53.6 us (9%)
  matrix products  52.5 us (8%)
  starting transfers between devices  27.9 us (4%)
  blocking collectives  15 us (2%)
  other arithmetic  14 us (2%)
  between operations  13.5 us (2%)
    all_to_all x1, waiting for transfers between devices, convert_sums_all_in(): lax.all_to_all(jnp.stack([my_tile for _ in range(lax.axis_size('dp'))], a...  244 us
    all_to_all x1, waiting for transfers between devices, shards(): lax.all_to_all(packed.reshape(groups, held_count, capacity, gathered.shap...  128 us
    all_to_all x1, waiting for transfers between devices, shards(): lax.all_to_all(expert_out[None], 'expert', split_axis=2, concat_axis=0, t...  74.2 us
    reshape x2, local copies, waits for them, and re-layouts, shards(): packed.reshape(groups, held_count, capacity, gathered.shape[1])  20.5 us
    dot_general x1, matrix products, shards(): jnp.einsum('erd,edf->erf', inputs, pieces[0], preferred_element_type=jnp....  19.2 us
    dot_general x1, matrix products, shards(): jnp.einsum('erd,edf->erf', inputs, pieces[1], preferred_element_type=jnp....  16.1 us
  transfers between devices with their start and end apart: 4, of which 3 were waited for; matrix products, arithmetic and copies ran while one was open for 7% of the time, Pallas kernels for 0%

profile of v1, /device:TPU:8, one launch (start us, length us, event | category | flops | bytes accessed | tf_op | source)
XLA Modules:
  0.0 622.1 jit_solution(11089278393356741661)
XLA Ops:
  6.5 6.1 pad_maximum_fusion
  12.7 0.9 copy-done.2
  13.6 5.0 all_to_all.45
  18.7 6.3 %stack.2 = bf16[4,2,768,1024]{3,2,1,0:T(8,128)(2,1)} broadcast(bf16[2,768,1024]{2,1,0:T(8,128)(2,1)S(1)} %copy-done), dimensions={1,2,3} | broadcast | bytes 15728640 | tf_op jit(solution)/shard_map/stack | solution.py:11
  25.0 9.8 %all-to-all-start.2 = ((bf16[4,2,768,1024]{3,2,1,0:T(8,128)(2,1)}), bf16[4,2,768,1024]{3,2,1,0:T(8,128)(2,1)}, u32[]{:S(2)}, u32[]{:S(2)}) async-start(bf16[4,2,768,1024]{3,2,1,0:T(8,128)(2,1)} %stack.2), calls=%async_computation.2 | async-start | bytes 25165824 | tf_op jit(solution)/shard_map/all_to_all | solution.py:10
  34.9 0.1 eq.43
  34.9 0.1 eq.39
  35.1 1.2 reduce-window.6
  36.3 0.2 slice_reduce_fusion
  36.5 0.1 fusion.14
  37.0 0.5 fusion.11
  37.5 4.6 convolution_convert_fusion.1
  42.2 9.9 %reshape.48 = bf16[32,2,12,4096]{3,2,1,0:T(8,128)(2,1)} reshape(bf16[768,4096]{1,0:T(8,128)(2,1)} %convolution_convert_fusion.1) | data formatting | bytes 12582912 | tf_op jit(solution)/shard_map/reshape | solution.py:76
  52.0 10.6 %copy.56 = bf16[32,2,12,4096]{3,1,2,0:T(2,128)(2,1)} copy(bf16[32,2,12,4096]{3,2,1,0:T(8,128)(2,1)} %reshape.48) | data formatting | bytes 12582912 | tf_op jit(solution)/shard_map/reshape | solution.py:76
  62.7 243.8 %all-to-all-done.2 = bf16[4,2,768,1024]{3,2,1,0:T(8,128)(2,1)} async-done(((bf16[4,2,768,1024]{3,2,1,0:T(8,128)(2,1)}), bf16[4,2,768,1024]{3,2,1,0:T(8,128)(2,1)}, u32[]{:S(2)}, u32[]{:S(2)}) %all-to-all-start.2) | async-done | bytes 12582944 | tf_op jit(solution)/shard_map/all_to_all | solution.py:10
  306.4 9.8 %all-to-all-start.1 = ((bf16[32,2,12,4096]{3,1,2,0:T(2,128)(2,1)}), bf16[32,2,12,4096]{3,1,2,0:T(2,128)(2,1)}, u32[]{:S(2)}, u32[]{:S(2)}) async-start(bf16[32,2,12,4096]{3,1,2,0:T(2,128)(2,1)} %copy.56), calls=%async_computation.1 | async-start | bytes 12582912 | tf_op jit(solution)/shard_map/all_to_all | solution.py:75
  316.3 10.7 %copy.68 = bf16[4,2,96,8,1024]{4,3,0,2,1:T(8,128)(2,1)} copy(bf16[4,2,96,8,1024]{4,3,2,1,0:T(8,128)(2,1)} %bitcast.19) | data formatting | bytes 25165824 | tf_op jit(solution)/shard_map/reshape | solution.py:9
  327.0 127.5 %all-to-all-done.1 = bf16[32,2,12,4096]{3,1,2,0:T(2,128)(2,1)} async-done(((bf16[32,2,12,4096]{3,1,2,0:T(2,128)(2,1)}), bf16[32,2,12,4096]{3,1,2,0:T(2,128)(2,1)}, u32[]{:S(2)}, u32[]{:S(2)}) %all-to-all-start.1) | async-done | bytes 6291488 | tf_op jit(solution)/shard_map/all_to_all | solution.py:75
  454.5 19.2 %fusion.2 = f32[2,384,768]{2,1,0:T(8,128)S(1)} fusion(bf16[4,4096,768]{2,1,0:T(8,128)(2,1)} %all-gather.2.cloned.1.call-done, bf16[2,384,4096]{2,0,1:T(2,128)(2,1)} %bitcast.4), kind=kOutput, calls=%fused_computation.2 | convolution fusion | flops 4831838208 | bytes 21233664 | tf_op jit(solution)/shard_map/erd,edf->erf/dot_general | solution.py:84
  473.7 16.1 %multiply_convert_fusion = bf16[2,384,768]{2,1,0:T(8,128)(2,1)S(1)} fusion(f32[2,384,768]{2,1,0:T(8,128)S(1)} %fusion.2, bf16[4,4096,768]{2,1,0:T(8,128)(2,1)} %all-gather.2.cloned.1.call-done, bf16[2,384,4096]{2,0,1:T(2,128)(2,1)} %bitcast.4), kind=kOutput, calls=%fused_computation.10 | convolution fusion | flops 4835377152 | bytes 22413312 | tf_op jit(solution)/shard_map/erd,edf->erf/dot_general | solution.py:85
  489.8 10.5 %convolution_convert_fusion = bf16[2,384,4096]{2,1,0:T(8,128)(2,1)S(1)} fusion(bf16[2,384,768]{2,1,0:T(8,128)(2,1)S(1)} %multiply_convert_fusion, bf16[2,768,4096]{2,1,0:T(8,128)(2,1)} %bitcast.50), kind=kOutput, calls=%fused_computation.4 | convolution fusion | flops 4834983936 | bytes 20054016 | tf_op jit(solution)/shard_map/erf,efd->erd/dot_general | solution.py:87
  500.3 1.1 copy.77
  501.4 10.0 %all_to_all.46 = bf16[2,2,384,2048]{3,2,1,0:T(8,128)(2,1)} all-to-all(bf16[2,2,384,2048]{3,2,1,0:T(8,128)(2,1)S(1)} %bitcast.51), channel_id=1, replica_groups=mesh['dp'=4,'expert'=32,'etp'=2] {'etp'}, dimensions={0} | all-to-all | bytes 12582912 | tf_op jit(solution)/shard_map/all_to_all | solution.py:50
  511.4 5.4 reduce_sum.32
  516.9 4.9 copy.62
  521.8 8.3 %all-to-all-start.4 = ((bf16[1,2,384,2048]{3,1,0,2:T(2,128)(2,1)}), bf16[1,2,384,2048]{3,1,0,2:T(2,128)(2,1)S(1)}, u32[]{:S(2)}, u32[]{:S(2)}) async-start(bf16[1,2,384,2048]{3,1,0,2:T(2,128)(2,1)} %copy.62), calls=%async_computation.4 | async-start | bytes 6291456 | tf_op jit(solution)/shard_map/all_to_all | solution.py:93
  530.2 0.5 select_reduce_fusion
  530.7 74.2 %all-to-all-done.4 = bf16[1,2,384,2048]{3,1,0,2:T(2,128)(2,1)S(1)} async-done(((bf16[1,2,384,2048]{3,1,0,2:T(2,128)(2,1)}), bf16[1,2,384,2048]{3,1,0,2:T(2,128)(2,1)S(1)}, u32[]{:S(2)}, u32[]{:S(2)}) %all-to-all-start.4) | async-done | bytes 3145760 | tf_op jit(solution)/shard_map/all_to_all | solution.py:93
  604.9 3.5 copy.63
  608.5 4.7 reshape.52
  613.2 0.7 fusion.17
  613.8 1.4 fusion.6
  (23 shorter events, 0.6 us)
Async XLA Ops:
  6.5 448.0 %all-gather.2.cloned.1.call-start = ((), (), s32[]{:S(2)}) async-start(), calls=%async_computation.5 | async-start | bytes 31457280 | tf_op jit(solution)/shard_map/all_gather | solution.py:39
  12.6 0.9 copy-start.2
  12.6 6.0 copy-start
  25.0 9.8 %copy-start.3 = (s32[64,8]{0,1:T(8,128)S(1)}, s32[64,8]{0,1:T(8,128)}, u32[]{:S(2)}) copy-start(s32[64,8]{0,1:T(8,128)} %param.7) | copy-start | bytes 6148
  25.0 11.9 %copy-start.1 = (bf16[2,64,2048]{2,1,0:T(8,128)(2,1)S(1)}, bf16[2,64,2048]{2,1,0:T(8,128)(2,1)}, u32[]{:S(2)}) copy-start(bf16[2,64,2048]{2,1,0:T(8,128)(2,1)} %all_to_all.45) | copy-start | bytes 1572868
  25.0 281.4 %all-to-all-start.2 = ((bf16[4,2,768,1024]{3,2,1,0:T(8,128)(2,1)}), bf16[4,2,768,1024]{3,2,1,0:T(8,128)(2,1)}, u32[]{:S(2)}, u32[]{:S(2)}) async-start(bf16[4,2,768,1024]{3,2,1,0:T(8,128)(2,1)} %stack.2), calls=%async_computation.2 | async-start | bytes 25165824 | tf_op jit(solution)/shard_map/all_to_all | solution.py:10
  306.4 148.1 %all-to-all-start.1 = ((bf16[32,2,12,4096]{3,1,2,0:T(2,128)(2,1)}), bf16[32,2,12,4096]{3,1,2,0:T(2,128)(2,1)}, u32[]{:S(2)}, u32[]{:S(2)}) async-start(bf16[32,2,12,4096]{3,1,2,0:T(2,128)(2,1)} %copy.56), calls=%async_computation.1 | async-start | bytes 12582912 | tf_op jit(solution)/shard_map/all_to_all | solution.py:75
  521.8 8.3 %copy-start.4 = (f32[64,8]{0,1:T(8,128)S(1)}, f32[64,8]{0,1:T(8,128)}, u32[]{:S(2)}) copy-start(f32[64,8]{0,1:T(8,128)} %param.8) | copy-start | bytes 6148
  521.8 83.2 %all-to-all-start.4 = ((bf16[1,2,384,2048]{3,1,0,2:T(2,128)(2,1)}), bf16[1,2,384,2048]{3,1,0,2:T(2,128)(2,1)S(1)}, u32[]{:S(2)}, u32[]{:S(2)}) async-start(bf16[1,2,384,2048]{3,1,0,2:T(2,128)(2,1)} %copy.62), calls=%async_computation.4 | async-start | bytes 6291456 | tf_op jit(solution)/shard_map/all_to_all | solution.py:93
Sparse Core Ops, SparseCore 0:
  12.8 361.8 all-gather.1
